TPU v7x, 8 devices: a whole 2x2x1 slice. The times are simulated.
8 devices in a mesh: dp: 2 (over y, z), ep: 4 (over x, core).
Axes of the slice: x: 2, y: 2, z: 1, core: 2. Of those that a mesh axis runs over, the one named last changes fastest.
Arguments:
- x: bfloat16 [2, 4, 256, 7168], P('dp', 'ep'), parts along dimension 0
- expert: int32 [2, 4, 256, 2], P('dp', 'ep'), parts along dimension 0
- slot: int32 [2, 4, 256, 2], P('dp', 'ep'), parts along dimension 0
- gate: float32 [2, 4, 256, 2], P('dp', 'ep'), parts along dimension 0
- w_gate: bfloat16 [8, 7168, 4864], P('ep')
- w_up: bfloat16 [8, 7168, 4864], P('ep')
- w_down: bfloat16 [8, 4864, 7168], P('ep')
Outputs:
- y: bfloat16 [2, 4, 256, 7168], P('dp', 'ep'), parts along dimension 0
There are 2 independent parts. A program takes and returns all parts, laid end to end along the dimension named above; an argument that names none is the same for every part.
All inputs are finite; a program needn't handle non-finite values.
Results may differ from a plain program's by a relative error of at most 0.009.
Values are sent between devices in bfloat16 or wider.
A program may use at most 2 GiB of HBM per device.

v0:
```python
import jax
import jax.numpy as jnp
from jax import lax
from jax.sharding import NamedSharding, PartitionSpec as P


def einsum(form, a, b):
    return jnp.einsum(form, a.astype(jnp.float32), b.astype(jnp.float32))


def solution(mesh):
    def placed(v, *spec):
        return lax.with_sharding_constraint(v, NamedSharding(mesh, P(*spec)))

    def step(x, expert, slot, gate, w_gate, w_up, w_down):
        experts, (tokens, top) = w_gate.shape[0], expert.shape[2:]
        slots = 5 * tokens * top // (4 * experts)
        to_expert = jax.nn.one_hot(expert, experts, dtype=jnp.bfloat16)
        to_slot = jax.nn.one_hot(slot, slots, dtype=jnp.bfloat16)
        weighted = to_expert * gate[..., None].astype(jnp.bfloat16)
        dispatch = einsum("abtke,abtkc->abtec", to_expert, to_slot).astype(jnp.bfloat16)
        combine = einsum("abtke,abtkc->abtec", weighted, to_slot).astype(jnp.bfloat16)
        z = einsum("abtec,abtd->aebcd", dispatch, x).astype(jnp.bfloat16)
        z = placed(z, "dp", None, "ep", None, None)
        z = placed(z, "dp", "ep", None, None, None)
        h = jax.nn.silu(einsum("aebcd,edf->aebcf", z, w_gate))
        h = (h * einsum("aebcd,edf->aebcf", z, w_up)).astype(jnp.bfloat16)
        out = einsum("aebcf,efd->aebcd", h, w_down).astype(jnp.bfloat16)
        out = placed(out, "dp", "ep", None, None, None)
        out = placed(out, "dp", None, "ep", None, None)
        y = einsum("abtec,aebcd->abtd", combine, out)
        return y.astype(jnp.bfloat16)

    return step
```

profile of v0, /device:TPU:0, one launch (start us, length us, event | category | flops | bytes accessed | tf_op | source)
XLA Modules:
  0.0 420.8 jit_solution(9802539620541959657)
XLA Ops:
  0.0 0.8 copy.11
  0.8 0.0 copy-start
  0.8 0.8 copy.9
  1.7 0.0 copy-start.2
  1.7 1.8 convolution_convert_fusion.1
  3.4 4.6 %convolution_convert_fusion = bf16[8,80,7168]{2,1,0:T(8,128)(2,1)S(1)} fusion(bf16[1,1,256,7168]{3,2,1,0:T(8,128)(2,1)} %param.3, bf16[256,8,80]{2,1,0:T(8,128)(2,1)S(1)} %convolution_convert_fusion.1), kind=kOutput, calls=%fused_computation.14 | convolution fusion | flops 2353397760 | bytes 13172736 | tf_op jit(solution)/abtec,abtd->aebcd/dot_general | solution.py:8
  8.1 106.4 %all-to-all.4 = bf16[1,4,2,1,80,7168]{5,4,2,3,0,1:T(8,128)(2,1)} all-to-all(bf16[1,4,2,1,80,7168]{5,4,2,3,0,1:T(8,128)(2,1)S(1)} %bitcast.99), channel_id=1, replica_groups=mesh['dp'=2,'ep'=4] {'ep'}, dimensions={1} | all-to-all | bytes 18350080 | tf_op jit(solution)/sharding_constraint;jit(solution)/sharding_constraint | solution.py:13
  114.5 0.0 copy-done
  114.5 0.0 copy-done.2
  114.5 59.3 %fusion.2 = f32[2,4,80,4864]{3,2,1,0:T(8,128)} fusion(bf16[2,7168,4864]{2,1,0:T(8,128)(2,1)} %param.5, bf16[1,4,2,1,80,7168]{5,4,2,3,0,1:T(8,128)(2,1)} %all-to-all.4), kind=kOutput, calls=%fused_computation.2 | convolution fusion | flops 44627394560 | bytes 161087488 | tf_op jit(solution)/aebcd,edf->aebcf/dot_general | solution.py:8
  173.8 59.2 %fusion.4 = f32[2,4,80,4864]{3,2,1,0:T(8,128)} fusion(bf16[2,7168,4864]{2,1,0:T(8,128)(2,1)} %param.4, bf16[1,4,2,1,80,7168]{5,4,2,3,0,1:T(8,128)(2,1)} %all-to-all.4), kind=kOutput, calls=%fused_computation.4 | convolution fusion | flops 44627394560 | bytes 161087488 | tf_op jit(solution)/aebcd,edf->aebcf/dot_general | solution.py:8
  233.0 64.4 %fusion.13 = bf16[1,2,4,1,80,7168]{5,4,2,1,3,0:T(8,128)(2,1)} fusion(bf16[2,4864,7168]{2,1,0:T(8,128)(2,1)} %param.6, f32[2,4,80,4864]{3,2,1,0:T(8,128)} %fusion.2, f32[2,4,80,4864]{3,2,1,0:T(8,128)} %fusion.4), kind=kOutput, calls=%fused_computation.15 | convolution fusion | flops 44650659840 | bytes 173539328 | tf_op jit(solution)/aebcf,efd->aebcd/dot_general | solution.py:8
  297.4 7.7 %copy.15 = bf16[1,2,4,1,80,7168]{5,4,1,3,0,2:T(8,128)(2,1)} copy(bf16[1,2,4,1,80,7168]{5,4,2,1,3,0:T(8,128)(2,1)} %fusion.13) | data formatting | bytes 18350080 | tf_op jit(solution)/sharding_constraint;jit(solution)/sharding_constraint | solution.py:13
  305.2 0.0 copy-start.4
  305.2 0.0 copy-start.1
  305.2 0.0 copy-start.3
  305.2 5.9 %all-to-all-start.1 = ((bf16[1,2,4,1,80,7168]{5,4,1,3,0,2:T(8,128)(2,1)}), bf16[1,2,4,1,80,7168]{5,4,1,3,0,2:T(8,128)(2,1)}, u32[]{:S(2)}, u32[]{:S(2)}) async-start(bf16[1,2,4,1,80,7168]{5,4,1,3,0,2:T(8,128)(2,1)} %copy.15), calls=%async_computation.1 | async-start | bytes 18350080 | tf_op jit(solution)/sharding_constraint;jit(solution)/sharding_constraint | solution.py:13
  311.1 0.0 copy-done.4
  311.1 0.1 copy.10
  311.2 0.0 copy-done.1
  311.2 0.0 copy-done.3
  311.2 2.2 convolution_convert_fusion.2
  313.5 98.9 %all-to-all-done.1 = bf16[1,2,4,1,80,7168]{5,4,1,3,0,2:T(8,128)(2,1)} async-done(((bf16[1,2,4,1,80,7168]{5,4,1,3,0,2:T(8,128)(2,1)}), bf16[1,2,4,1,80,7168]{5,4,1,3,0,2:T(8,128)(2,1)}, u32[]{:S(2)}, u32[]{:S(2)}) %all-to-all-start.1) | async-done | bytes 9175072 | tf_op jit(solution)/sharding_constraint;jit(solution)/sharding_constraint | solution.py:13
  412.3 8.5 %fusion.19 = bf16[1,1,256,7168]{3,2,1,0:T(8,128)(2,1)} fusion(bf16[8,80,7168]{2,1,0:T(8,128)(2,1)} %bitcast.25, bf16[256,8,80]{2,1,0:T(8,128)(2,1)S(1)} %convolution_convert_fusion.2), kind=kOutput, calls=%fused_computation.20 | convolution fusion | flops 2350645248 | bytes 13172736 | tf_op jit(solution)/abtec,aebcd->abtd/dot_general | solution.py:8
  (1 shorter events, 0.0 us)
Async XLA Ops:
  0.8 113.7 %copy-start = (s32[256,2]{1,0:T(8,128)}, s32[256,2]{1,0:T(8,128)S(1)}, u32[]{:S(2)}) copy-start(s32[256,2]{1,0:T(8,128)S(1)} %copy.11) | copy-start | bytes 6148
  1.7 112.9 %copy-start.2 = (s32[256,2]{1,0:T(8,128)}, s32[256,2]{1,0:T(8,128)S(1)}, u32[]{:S(2)}) copy-start(s32[256,2]{1,0:T(8,128)S(1)} %copy.9) | copy-start | bytes 6148
  305.2 5.9 %copy-start.4 = (f32[1,1,256,2]{2,3,1,0:T(2,128)S(1)}, f32[1,1,256,2]{2,3,1,0:T(2,128)}, u32[]{:S(2)}) copy-start(f32[1,1,256,2]{2,3,1,0:T(2,128)} %param.1) | copy-start | bytes 6148
  305.2 6.1 %copy-start.1 = (s32[256,2]{1,0:T(8,128)S(1)}, s32[256,2]{1,0:T(8,128)}, u32[]{:S(2)}) copy-start(s32[256,2]{1,0:T(8,128)} %copy-done) | copy-start | bytes 6148
  305.2 6.1 %copy-start.3 = (s32[256,2]{1,0:T(8,128)S(1)}, s32[256,2]{1,0:T(8,128)}, u32[]{:S(2)}) copy-start(s32[256,2]{1,0:T(8,128)} %copy-done.2) | copy-start | bytes 6148
  305.2 107.1 %all-to-all-start.1 = ((bf16[1,2,4,1,80,7168]{5,4,1,3,0,2:T(8,128)(2,1)}), bf16[1,2,4,1,80,7168]{5,4,1,3,0,2:T(8,128)(2,1)}, u32[]{:S(2)}, u32[]{:S(2)}) async-start(bf16[1,2,4,1,80,7168]{5,4,1,3,0,2:T(8,128)(2,1)} %copy.15), calls=%async_computation.1 | async-start | bytes 18350080 | tf_op jit(solution)/sharding_constraint;jit(solution)/sharding_constraint | solution.py:13
where the time goes:
time: 421 us
  matrix products  200 us (48%)
  blocking collectives  106 us (25%)
  waiting for transfers between devices  98.9 us (23%)
  local copies, waits for them, and re-layouts  9.55 us (2%)
  starting transfers between devices  5.89 us (1%)
    dot_general x7, matrix products, einsum(): return jnp.einsum(form, a.astype(jnp.float32), b.astype(jnp.float32))  200 us
    another operation x1, blocking collectives, placed(): return lax.with_sharding_constraint(v, NamedSharding(mesh, P(*spec)))  106 us
    another operation x1, waiting for transfers between devices, placed(): return lax.with_sharding_constraint(v, NamedSharding(mesh, P(*spec)))  98.9 us
  transfers between devices with their start and end apart: 1, of which 1 were waited for; matrix products, arithmetic and copies ran while one was open for 1% of the time, Pallas kernels for 0%

commit v1 on v0

v1 whole, which is shorter than its diff:
```python
import functools

import jax
import jax.numpy as jnp
from jax import lax
from jax.experimental import pallas as pl
from jax.experimental.pallas import tpu as pltpu
from jax.sharding import PartitionSpec as P

MESH = pl.DeviceIdType.MESH
TOK, D, FF, SLOTS = 256, 7168, 4864, 80
ROWS = 4 * SLOTS
KC = 512
NK = D // KC
NT = FF // 256
NC = 512
NN = D // NC
NS = 4
LAG = 3
RING = 4
RINGX = 5
BF, F32 = jnp.bfloat16, jnp.float32


def kernel(x, u, meta, wg, wu, wd, y, xin,
           acc, wbuf, h, z, xs, oh, ct, mrecv, obuf, send3, send1, sendx, y3r, y1r, yxr, yout,
           wsem, lsem, osem, msend, mrsem, csend, crecv, ssend, srecv, fsend, frecv,
           s3, r3, s1, r1, sx, rx):
    me = lax.axis_index("ep")
    pair = me // 2
    sib = pair * 2 + (1 - lax.rem(me, 2))
    far = (1 - pair) * 2 + lax.rem(me, 2)
    diag = (1 - pair) * 2 + (1 - lax.rem(me, 2))
    peers = (sib, far, diag)

    def remote(src, dst, send, recv, to):
        return pltpu.make_async_remote_copy(
            src_ref=src, dst_ref=dst, send_sem=send, recv_sem=recv, device_id={"ep": to}, device_id_type=MESH)

    def kcols(k):
        return pl.ds(pl.multiple_of(k * KC, KC), KC)

    def w1(k, e, m):
        return pltpu.make_async_copy((wg, wu)[m].at[e, kcols(k), :], wbuf.at[2 * e + m], wsem.at[2 * e + m, 0])

    def w2(j):
        n, e, slot = j // 2, lax.rem(j, 2), lax.rem(j, NS)
        col = pl.multiple_of(n * NC, NC)
        out = []
        for b in range(NT // 2):
            out.append(pltpu.make_async_copy(
                wd.at[e, b * 512:(b + 1) * 512, pl.ds(col, NC)],
                wbuf.at[slot, :, b * 512:(b + 1) * 512], wsem.at[slot, b]))
        for q in range(2):
            out.append(pltpu.make_async_copy(
                wd.at[e, FF - 256:, pl.ds(pl.multiple_of(col + q * 256, 256), 256)],
                wbuf.at[slot, q * 256:(q + 1) * 256, FF - 256:], wsem.at[slot, NT // 2 + q]))
        return out

    for m in range(2):
        w1(0, 0, m).start()

    barrier = pltpu.get_barrier_semaphore()
    for p in peers:
        pl.semaphore_signal(barrier, inc=1, device_id={"ep": p}, device_id_type=MESH)
    pl.semaphore_wait(barrier, 3)

    def cross(k):
        return remote(u.at[:, kcols(k)], xin.at[1, :, kcols(k)], csend.at[k], crecv.at[k], far)

    def side(k):
        return remote(x.at[:, kcols(k)], xin.at[0, :, kcols(k)], ssend.at[k], srecv.at[k], sib)

    def forward(k):
        return remote(xin.at[1, :, kcols(k)], xin.at[2, :, kcols(k)], fsend.at[k], frecv.at[k], sib)

    def metas(i):
        return remote(meta.at[peers[i]], mrecv.at[i], msend.at[i], mrsem.at[i], peers[i])

    def loads(k, slot):
        return [pltpu.make_async_copy(src.at[:, kcols(k)], xs.at[slot, i], lsem.at[slot, i])
                for i, src in enumerate((x, xin.at[0], xin.at[1], xin.at[2]))]

    for i in range(3):
        metas(i).start()
    mine = pltpu.make_async_copy(meta.at[me], mrecv.at[3], lsem.at[0, 0])
    mine.start()

    def start_x(k, _):
        cross(k).start()
        side(k).start()
        return 0
    lax.fori_loop(0, NK, start_x, 0)

    acc[...] = jnp.zeros_like(acc)
    obuf[...] = jnp.zeros_like(obuf)
    mine.wait()
    row = lax.broadcasted_iota(jnp.int32, (SLOTS, TOK), 0).astype(F32)
    for s in range(4):
        if s > 0:
            metas(s - 1).wait_recv()
        src = (s - 1) % 4
        parts = []
        for e in range(2):
            hit = row == mrecv[src, e:e + 1, :]
            oh[s, e * SLOTS:(e + 1) * SLOTS, :] = jnp.where(hit, 1.0, 0.0).astype(BF)
            parts.append(jnp.where(hit, mrecv[src, 2 + e:3 + e, :], 0.0))
        full = jnp.concatenate(parts + [jnp.zeros((256 - 2 * SLOTS, TOK), F32)], axis=0)
        ct[s] = jnp.transpose(full).astype(BF)

    def dot(lhs, rhs):
        return jnp.dot(lhs, rhs, preferred_element_type=F32)

    def select(xslot, zslot):
        for s in range(4):
            got = dot(oh[s], xs[xslot, s]).astype(BF)
            for e in range(2):
                z[zslot, e, s * SLOTS:(s + 1) * SLOTS, :] = got[e * SLOTS:(e + 1) * SLOTS]

    def block(zslot, e):
        for c in range(0, FF, 1280):
            cols = slice(c, min(c + 1280, FF))
            for m in range(2):
                acc[e, m, :, cols] += dot(z[zslot, e], wbuf[2 * e + m, :, cols])

    for k in range(2):
        cross(k).wait_recv()
        forward(k).start()
    side(0).wait_recv()
    forward(0).wait_recv()
    for c in loads(0, 0):
        c.start()
    for c in loads(0, 0):
        c.wait()
    select(0, 0)

    def step(k, _):
        now, later = lax.rem(k, 2), lax.rem(k + 1, 2)

        @pl.when(k + 1 < NK)
        def _():
            side(k + 1).wait_recv()
            forward(k + 1).wait_recv()
            for c in loads(k + 1, later):
                c.start()
        for m in range(2):
            w1(k, 1, m).start()
        for m in range(2):
            w1(k, 0, m).wait()
        block(now, 0)

        @pl.when(k + 1 < NK)
        def _():
            for m in range(2):
                w1(k + 1, 0, m).start()
            for c in loads(k + 1, later):
                c.wait()

        @pl.when(k + 2 < NK)
        def _():
            cross(k + 2).wait_recv()
            forward(k + 2).start()
        for m in range(2):
            w1(k, 1, m).wait()
        block(now, 1)
        select(later, later)
        return 0

    lax.fori_loop(0, NK, step, 0)

    for j in range(NS):
        for c in w2(j):
            c.start()

    def act(i, _):
        e = i // NT
        cols = pl.ds(pl.multiple_of(lax.rem(i, NT) * 256, 256), 256)
        g = acc[e, 0, :, cols]
        h[e, :, cols] = (jax.nn.silu(g) * acc[e, 1, :, cols]).astype(BF)
        return 0
    lax.fori_loop(0, 2 * NT, act, 0)

    def held(which, n):
        return (which, n // 9, slice(0, TOK), pl.ds(pl.multiple_of(lax.rem(n, 9) * NC, NC), NC))

    def ncols(n):
        return pl.ds(pl.multiple_of(n * NC, NC), NC)

    def to3(n):
        b, r = lax.rem(n, 2), lax.rem(n, RING)
        return remote(send3.at[b], y3r.at[r], s3.at[b], r3.at[r], sib)

    def to1(n):
        b, r = lax.rem(n, 2), lax.rem(n, RING)
        return remote(send1.at[b], y1r.at[r], s1.at[b], r1.at[r], sib)

    def tox(n):
        b, r = lax.rem(n, 2), lax.rem(n, RINGX)
        return remote(sendx.at[b], yxr.at[r], sx.at[b], rx.at[r], far)

    def out(n):
        b = lax.rem(n, 2)
        return pltpu.make_async_copy(yout.at[b], y.at[:, ncols(n)], osem.at[b])

    def chip_sum(n):
        b, r = lax.rem(n, 2), lax.rem(n, RING)
        sendx[b] = (acc[held(1, n)] + y3r[r].astype(F32)).astype(BF)

    def assemble(n):
        b, r = lax.rem(n, 2), lax.rem(n, RING)
        yout[b] = (acc[held(0, n)] + y1r[r].astype(F32) + yxr[lax.rem(n, RINGX)].astype(F32)).astype(BF)

    def down(e, slot):
        tail = jnp.concatenate([wbuf[slot, q * 256:(q + 1) * 256, FF - 256:] for q in range(2)], axis=1)
        tiles = [wbuf[slot, :, b * 512:(b + 1) * 512] for b in range(NT // 2)] + [tail]
        got = dot(h[e], jnp.concatenate(tiles, axis=0)).astype(BF)
        for s in range(4):
            obuf[s, e * SLOTS:(e + 1) * SLOTS, :] = got[s * SLOTS:(s + 1) * SLOTS]

    def combine(n):
        b = lax.rem(n, 2)
        send3[b] = dot(ct[3], obuf[3]).astype(BF)
        send1[b] = dot(ct[1], obuf[1]).astype(BF)
        acc[held(1, n)] = dot(ct[2], obuf[2])
        acc[held(0, n)] = dot(ct[0], obuf[0])

    def step(n, _):
        @pl.when(n >= 1)
        def _():
            @pl.when(2 * n + 3 < 2 * NN)
            def _():
                for c in w2(2 * n + 3):
                    c.start()

        @pl.when(n >= LAG)
        def _():
            to1(n - LAG).wait_recv()
            tox(n - LAG).wait_recv()

            @pl.when(n >= LAG + 2)
            def _():
                out(n - LAG - 2).wait()
            assemble(n - LAG)
            out(n - LAG).start()
        for c in w2(2 * n):
            c.wait()
        down(0, lax.rem(2 * n, NS))

        @pl.when(2 * n + 4 < 2 * NN)
        def _():
            for c in w2(2 * n + 4):
                c.start()

        @pl.when(n >= 1)
        def _():
            to3(n - 1).wait_recv()

            @pl.when(n >= 3)
            def _():
                tox(n - 3).wait_send()
            chip_sum(n - 1)
            tox(n - 1).start()

        @pl.when(n >= 2)
        def _():
            to3(n - 2).wait_send()
            to1(n - 2).wait_send()
        for c in w2(2 * n + 1):
            c.wait()
        down(1, lax.rem(2 * n + 1, NS))
        combine(n)
        to3(n).start()
        to1(n).start()
        return 0

    lax.fori_loop(0, NN, step, 0)

    last = NN - 1
    to3(last).wait_recv()
    tox(last - 2).wait_send()
    chip_sum(last)
    tox(last).start()
    for n in range(NN - LAG, NN):
        to1(n).wait_recv()
        tox(n).wait_recv()
        out(n - 2).wait()
        assemble(n)
        out(n).start()
    for n in range(NN - 2, NN):
        out(n).wait()
        tox(n).wait_send()
        to3(n).wait_send()
        to1(n).wait_send()

    def drain(k, _):
        cross(k).wait_send()
        side(k).wait_send()
        forward(k).wait_send()
        return 0
    lax.fori_loop(0, NK, drain, 0)
    for i in range(3):
        metas(i).wait_send()


def layer(x, u, meta, wg, wu, wd):
    hbm, vmem, dma = pl.BlockSpec(memory_space=pl.ANY), pltpu.VMEM, pltpu.SemaphoreType.DMA
    chunk = (TOK, NC)
    return pl.pallas_call(
        kernel,
        out_shape=(jax.ShapeDtypeStruct((TOK, D), BF), jax.ShapeDtypeStruct((3, TOK, D), BF)),
        in_specs=[hbm] * 6,
        out_specs=(hbm, hbm),
        scratch_shapes=[
            vmem((2, 2, ROWS, FF), F32),
            vmem((NS, KC, FF), BF),
            vmem((2, ROWS, FF), BF),
            vmem((2, 2, ROWS, KC), BF),
            vmem((2, 4, TOK, KC), BF),
            vmem((4, 2 * SLOTS, TOK), BF),
            vmem((4, TOK, 256), BF),
            vmem((4, 8, TOK), F32),
            vmem((4, 256, NC), BF),
            vmem((2, *chunk), BF),
            vmem((2, *chunk), BF),
            vmem((2, *chunk), BF),
            vmem((RING, *chunk), BF),
            vmem((RING, *chunk), BF),
            vmem((RINGX, *chunk), BF),
            vmem((2, *chunk), BF),
            dma((NS, NT // 2 + 2)), dma((2, 4)), dma((2,)), dma((3,)), dma((3,)),
            dma((NK,)), dma((NK,)), dma((NK,)), dma((NK,)), dma((NK,)), dma((NK,)),
            dma((2,)), dma((RING,)), dma((2,)), dma((RING,)), dma((2,)), dma((RINGX,)),
        ],
        compiler_params=pltpu.CompilerParams(
            collective_id=0, has_side_effects=True, vmem_limit_bytes=67043328),
        name="moe",
    )(x, u, meta, wg, wu, wd)


def solution(mesh):
    def body(x, expert, slot, gate, wg, wu, wd):
        x = x[0, 0]
        expert, slot, gate = expert[0, 0], slot[0, 0], gate[0, 0].astype(BF).astype(F32)
        experts = 2 * mesh.shape["ep"]
        chosen = (expert.T[None] == jnp.arange(experts)[:, None, None]) & (slot.T[None] < SLOTS)
        pos = jnp.sum(jnp.where(chosen, slot.T[None] + 1, 0), axis=1).astype(F32) - 1.0
        weight = jnp.sum(jnp.where(chosen, gate.T[None], 0.0), axis=1)
        meta = jnp.concatenate(
            [pos.reshape(-1, 2, TOK), weight.reshape(-1, 2, TOK), jnp.zeros((experts // 2, 4, TOK), F32)], axis=1)
        return layer(x, x, meta, wg, wu, wd)[0][None, None]

    tok = P("dp", "ep", None, None)
    ex = P("ep", None, None)
    with jax.sharding.use_abstract_mesh(mesh.abstract_mesh):
        return jax.shard_map(
            body, mesh=mesh, in_specs=(tok, tok, tok, tok, ex, ex, ex), out_specs=tok, check_vma=False)
```

time: 421 us -> 228 us (0.54)
  Pallas kernels: 0 us -> 220 us
  matrix products: 200 us -> 0 us
  blocking collectives: 106 us -> 0 us
  waiting for transfers between devices: 98.9 us -> 0 us
  starting transfers between devices: 5.89 us -> 0 us
  local copies, waits for them, and re-layouts: 9.55 us -> 4.22 us
    pallas_call x0 -> x1, Pallas kernels: none -> 220 us  [layer(): pl.pallas_call(kernel, out_shape=(jax.ShapeDtypeStruct((TOK, D), BF), jax...]
    dot_general x7 -> x0, matrix products: 200 us -> none  [einsum(): return jnp.einsum(form, a.astype(jnp.float32), b.astype(jnp.float32))]
    another operation x1 -> x0, blocking collectives: 106 us -> none  [placed(): return lax.with_sharding_constraint(v, NamedSharding(mesh, P(*spec)))]
    another operation x1 -> x0, waiting for transfers between devices: 98.9 us -> none  [placed(): return lax.with_sharding_constraint(v, NamedSharding(mesh, P(*spec)))]
    another operation x1 -> x0, local copies, waits for them, and re-layouts: 7.74 us -> none  [placed(): return lax.with_sharding_constraint(v, NamedSharding(mesh, P(*spec)))]
    another operation x1 -> x0, starting transfers between devices: 5.89 us -> none  [placed(): return lax.with_sharding_constraint(v, NamedSharding(mesh, P(*spec)))]
  transfers between devices with their start and end apart: 1 -> 0, of which waited for: 1 -> 0; matrix products, arithmetic and copies ran while one was open for 1% -> 0% of each run, Pallas kernels for 0% -> 0%
where the time goes in v1:
time: 228 us
  Pallas kernels  220 us (96%)
  local copies, waits for them, and re-layouts  4.22 us (2%)
  other arithmetic  4.13 us (2%)
    pallas_call x1, Pallas kernels, layer(): pl.pallas_call(kernel, out_shape=(jax.ShapeDtypeStruct((TOK, D), BF), jax...  220 us

profile of v1, /device:TPU:0, one launch (start us, length us, event | category | flops | bytes accessed | tf_op | source)
XLA Modules:
  0.0 228.0 jit_solution(6652895764609291008)
XLA Ops:
  0.0 0.1 pad.2.clone
  0.1 0.7 compare_bitcast_fusion
  0.8 0.7 convert_bitcast_fusion
  1.4 0.7 add_bitcast_fusion
  2.1 0.7 select_reduce_fusion.1
  2.8 0.7 select_reduce_fusion
  3.6 0.7 maximum_maximum_fusion.meta
  4.2 219.7 %moe.1 = (bf16[256,7168]{1,0:T(8,128)(2,1)}, bf16[3,256,7168]{2,1,0:T(8,128)(2,1)}) custom-call(bf16[256,7168]{1,0:T(8,128)(2,1)} %bitcast.18, bf16[256,7168]{1,0:T(8,128)(2,1)} %bitcast.19, f32[4,8,256]{2,1,0:T(8,128)} %maximum_maximum_fusion.meta, bf16[2,7168,4864]{2,1,0:T(8,128)(2,1)} %wg.1, bf16[2,7168,4864]{2,1,0:T(8,128)(2,1)} %wu.1, ...), custom_call_target="tpu_custom_call" | custom-call | tf_op jit(solution)/shard_map/moe/pallas_call | solution.py:308
  223.9 4.1 %copy.9 = bf16[1,1,256,7168]{3,2,1,0:T(8,128)(2,1)} copy(bf16[1,1,256,7168]{3,2,1,0:T(8,128)(2,1)} %bitcast.20) | data formatting | bytes 7340032
  (4 shorter events, 0.0 us)

commit v2 on v1

--- a/solution.py
+++ b/solution.py
@@ -19,19 +19,24 @@
 LAG = 3
 RING = 4
 RINGX = 5
+PACKED = 176
 BF, F32 = jnp.bfloat16, jnp.float32
 
 
-def kernel(x, u, meta, wg, wu, wd, y, xin,
-           acc, wbuf, h, z, xs, oh, ct, mrecv, obuf, send3, send1, sendx, y3r, y1r, yxr, yout,
+def kernel(rows, x, meta, wg, wu, wd, y, xin,
+           acc, wbuf, h, z, xs, oh, ct, mown, pack, mrecv, obuf, send3, send1, sendx, y3r, y1r, yxr, yout, perm,
            wsem, lsem, osem, msend, mrsem, csend, crecv, ssend, srecv, fsend, frecv,
            s3, r3, s1, r1, sx, rx):
+    packed = rows < TOK
     me = lax.axis_index("ep")
     pair = me // 2
     sib = pair * 2 + (1 - lax.rem(me, 2))
     far = (1 - pair) * 2 + lax.rem(me, 2)
     diag = (1 - pair) * 2 + (1 - lax.rem(me, 2))
     peers = (sib, far, diag)
+
+    def dot(lhs, rhs):
+        return jnp.dot(lhs, rhs, preferred_element_type=F32)
 
     def remote(src, dst, send, recv, to):
         return pltpu.make_async_remote_copy(
@@ -57,59 +62,108 @@
                 wbuf.at[slot, q * 256:(q + 1) * 256, FF - 256:], wsem.at[slot, NT // 2 + q]))
         return out
 
+    def packed_x(k):
+        return h.at[k // 9, :rows, pl.ds(pl.multiple_of(lax.rem(k, 9) * KC, KC), KC)]
+
+    def cross(k):
+        src = packed_x(k) if packed else x.at[:, kcols(k)]
+        return remote(src, xin.at[1, :rows, kcols(k)], csend.at[k], crecv.at[k], far)
+
+    def side(k):
+        return remote(x.at[:, kcols(k)], xin.at[0, :, kcols(k)], ssend.at[k], srecv.at[k], sib)
+
+    def forward(k):
+        return remote(xin.at[1, :rows, kcols(k)], xin.at[2, :rows, kcols(k)], fsend.at[k], frecv.at[k], sib)
+
+    def metas(i):
+        src = pack.at[pl.ds(pl.multiple_of(peers[i] * 8, 8), 8)] if packed and i else meta.at[peers[i]]
+        return remote(src, mrecv.at[i], msend.at[i], mrsem.at[i], peers[i])
+
+    def loads(k, slot):
+        return [pltpu.make_async_copy(src.at[:r, kcols(k)], xs.at[slot, i, :r], lsem.at[slot, i])
+                for i, (src, r) in enumerate(((x, TOK), (xin.at[0], TOK), (xin.at[1], rows), (xin.at[2], rows)))]
+
     for m in range(2):
         w1(0, 0, m).start()
-
+    mine = pltpu.make_async_copy(meta, mown, lsem.at[0, 0])
+    mine.start()
+    if packed:
+        halves = [pltpu.make_async_copy(x.at[:, c:c + w], wbuf.at[2 + i, :TOK, :w], lsem.at[1, i])
+                  for i, (c, w) in enumerate(((0, 9 * KC), (9 * KC, D - 9 * KC)))]
+        for c in halves:
+            c.start()
     barrier = pltpu.get_barrier_semaphore()
     for p in peers:
         pl.semaphore_signal(barrier, inc=1, device_id={"ep": p}, device_id_type=MESH)
+    mine.wait()
+
+    def pack_x(k):
+        src = wbuf[2 + k // 9, :TOK, pl.ds(pl.multiple_of(lax.rem(k, 9) * KC, KC), KC)]
+        packed_x(k)[...] = dot(perm[0, :rows], src).astype(BF)
+
+    if packed:
+        need = jnp.zeros((1, TOK), F32)
+        for t in range(2):
+            there = mown[(1 - pair) * 2 + t]
+            need = jnp.maximum(need, jnp.maximum(there[0:1], there[1:2]))
+        need = jnp.where(need > 0.0, 1.0, 0.0)
+        r_at = lax.broadcasted_iota(jnp.int32, (TOK, TOK), 0)
+        c_at = lax.broadcasted_iota(jnp.int32, (TOK, TOK), 1)
+        before = jnp.where(r_at < c_at, 1.0, 0.0).astype(BF)
+        rank = dot(jnp.broadcast_to(need, (16, TOK)).astype(BF), before)[0:1]
+        rank = jnp.where(need > 0.0, rank, -1.0)
+        to_row = jnp.where(r_at.astype(F32) == rank, 1.0, 0.0)
+        perm[0] = to_row.astype(BF)
+        for c in halves:
+            c.wait()
+        pack_x(0)
+        perm[1] = jnp.transpose(to_row).astype(BF)
+        pack[...] = dot(mown[...].reshape(4 * 8, TOK).astype(BF), perm[1])
     pl.semaphore_wait(barrier, 3)
-
-    def cross(k):
-        return remote(u.at[:, kcols(k)], xin.at[1, :, kcols(k)], csend.at[k], crecv.at[k], far)
-
-    def side(k):
-        return remote(x.at[:, kcols(k)], xin.at[0, :, kcols(k)], ssend.at[k], srecv.at[k], sib)
-
-    def forward(k):
-        return remote(xin.at[1, :, kcols(k)], xin.at[2, :, kcols(k)], fsend.at[k], frecv.at[k], sib)
-
-    def metas(i):
-        return remote(meta.at[peers[i]], mrecv.at[i], msend.at[i], mrsem.at[i], peers[i])
-
-    def loads(k, slot):
-        return [pltpu.make_async_copy(src.at[:, kcols(k)], xs.at[slot, i], lsem.at[slot, i])
-                for i, src in enumerate((x, xin.at[0], xin.at[1], xin.at[2]))]
-
+    cross(0).start()
     for i in range(3):
         metas(i).start()
-    mine = pltpu.make_async_copy(meta.at[me], mrecv.at[3], lsem.at[0, 0])
-    mine.start()
+    side(0).start()
 
     def start_x(k, _):
-        cross(k).start()
-        side(k).start()
-        return 0
-    lax.fori_loop(0, NK, start_x, 0)
-
-    acc[...] = jnp.zeros_like(acc)
+        if packed:
+            @pl.when(k < NK)
+            def _():
+                pack_x(k)
+
+            @pl.when(k > 1)
+            def _():
+                cross(k - 1).start()
+                side(k - 1).start()
+        else:
+            cross(k).start()
+            side(k).start()
+        return 0
+    lax.fori_loop(1, NK + 1 if packed else NK, start_x, 0)
+    if packed:
+        for i in range(2):
+            xs[i, 2:, rows:] = jnp.zeros((2, TOK - rows, KC), BF)
+        yxr[:, rows:] = jnp.zeros((RINGX, TOK - rows, NC), BF)
+
+    def clear(i, _):
+        acc[i // 40, lax.rem(i // 20, 2), pl.ds(pl.multiple_of(lax.rem(i, 20) * 16, 16), 16), :] = jnp.zeros((16, FF), F32)
+        return 0
+    lax.fori_loop(0, 80, clear, 0)
     obuf[...] = jnp.zeros_like(obuf)
-    mine.wait()
-    row = lax.broadcasted_iota(jnp.int32, (SLOTS, TOK), 0).astype(F32)
+    row = lax.broadcasted_iota(jnp.int32, (SLOTS, TOK), 0).astype(F32) + 1.0
     for s in range(4):
         if s > 0:
             metas(s - 1).wait_recv()
-        src = (s - 1) % 4
+            got = mrecv[s - 1]
+        else:
+            got = mown[me]
         parts = []
         for e in range(2):
-            hit = row == mrecv[src, e:e + 1, :]
+            hit = row == got[e:e + 1]
             oh[s, e * SLOTS:(e + 1) * SLOTS, :] = jnp.where(hit, 1.0, 0.0).astype(BF)
-            parts.append(jnp.where(hit, mrecv[src, 2 + e:3 + e, :], 0.0))
+            parts.append(jnp.where(hit, got[2 + e:3 + e], 0.0))
         full = jnp.concatenate(parts + [jnp.zeros((256 - 2 * SLOTS, TOK), F32)], axis=0)
         ct[s] = jnp.transpose(full).astype(BF)
-
-    def dot(lhs, rhs):
-        return jnp.dot(lhs, rhs, preferred_element_type=F32)
 
     def select(xslot, zslot):
         for s in range(4):
@@ -117,15 +171,18 @@
             for e in range(2):
                 z[zslot, e, s * SLOTS:(s + 1) * SLOTS, :] = got[e * SLOTS:(e + 1) * SLOTS]
 
-    def block(zslot, e):
+    def block(zslot, e, last):
         for c in range(0, FF, 1280):
             cols = slice(c, min(c + 1280, FF))
-            for m in range(2):
-                acc[e, m, :, cols] += dot(z[zslot, e], wbuf[2 * e + m, :, cols])
-
-    for k in range(2):
-        cross(k).wait_recv()
-        forward(k).start()
+            g, v = (acc[e, m, :, cols] + dot(z[zslot, e], wbuf[2 * e + m, :, cols]) for m in range(2))
+            if last:
+                h[e, :, cols] = (jax.nn.silu(g) * v).astype(BF)
+            else:
+                acc[e, 0, :, cols] = g
+                acc[e, 1, :, cols] = v
+
+    cross(0).wait_recv()
+    forward(0).start()
     side(0).wait_recv()
     forward(0).wait_recv()
     for c in loads(0, 0):
@@ -134,20 +191,32 @@
         c.wait()
     select(0, 0)
 
+    def arrived(k, slot):
+        side(k).wait_recv()
+        forward(k).wait_recv()
+        for c in loads(k, slot):
+            c.start()
+
     def step(k, _):
         now, later = lax.rem(k, 2), lax.rem(k + 1, 2)
-
-        @pl.when(k + 1 < NK)
-        def _():
-            side(k + 1).wait_recv()
-            forward(k + 1).wait_recv()
-            for c in loads(k + 1, later):
-                c.start()
         for m in range(2):
             w1(k, 1, m).start()
+
+        @pl.when(k == 0)
+        def _():
+            cross(1).wait_recv()
+            forward(1).start()
+
+        @pl.when(jnp.logical_and(k > 0, k + 1 < NK))
+        def _():
+            arrived(k + 1, later)
         for m in range(2):
             w1(k, 0, m).wait()
-        block(now, 0)
+        block(now, 0, False)
+
+        @pl.when(k == 0)
+        def _():
+            arrived(1, 1)
 
         @pl.when(k + 1 < NK)
         def _():
@@ -162,13 +231,29 @@
             forward(k + 2).start()
         for m in range(2):
             w1(k, 1, m).wait()
-        block(now, 1)
+        block(now, 1, False)
         select(later, later)
         return 0
 
-    lax.fori_loop(0, NK, step, 0)
-
-    for j in range(NS):
+    lax.fori_loop(0, NK - 1 if packed else NK, step, 0)
+    if packed:
+        def sent(k, _):
+            cross(k).wait_send()
+            return 0
+        lax.fori_loop(0, NK, sent, 0)
+        for m in range(2):
+            w1(NK - 1, 1, m).start()
+        for m in range(2):
+            w1(NK - 1, 0, m).wait()
+        block((NK - 1) % 2, 0, True)
+        for j in range(2):
+            for c in w2(j):
+                c.start()
+        for m in range(2):
+            w1(NK - 1, 1, m).wait()
+        block((NK - 1) % 2, 1, True)
+
+    for j in range(2 if packed else 0, NS):
         for c in w2(j):
             c.start()
 
@@ -178,10 +263,11 @@
         g = acc[e, 0, :, cols]
         h[e, :, cols] = (jax.nn.silu(g) * acc[e, 1, :, cols]).astype(BF)
         return 0
-    lax.fori_loop(0, 2 * NT, act, 0)
+    if not packed:
+        lax.fori_loop(0, 2 * NT, act, 0)
 
     def held(which, n):
-        return (which, n // 9, slice(0, TOK), pl.ds(pl.multiple_of(lax.rem(n, 9) * NC, NC), NC))
+        return (which, n // 9, slice(0, rows if which else TOK), pl.ds(pl.multiple_of(lax.rem(n, 9) * NC, NC), NC))
 
     def ncols(n):
         return pl.ds(pl.multiple_of(n * NC, NC), NC)
@@ -196,7 +282,7 @@
 
     def tox(n):
         b, r = lax.rem(n, 2), lax.rem(n, RINGX)
-        return remote(sendx.at[b], yxr.at[r], sx.at[b], rx.at[r], far)
+        return remote(sendx.at[b], yxr.at[r, :rows], sx.at[b], rx.at[r], far)
 
     def out(n):
         b = lax.rem(n, 2)
@@ -208,7 +294,9 @@
 
     def assemble(n):
         b, r = lax.rem(n, 2), lax.rem(n, RING)
-        yout[b] = (acc[held(0, n)] + y1r[r].astype(F32) + yxr[lax.rem(n, RINGX)].astype(F32)).astype(BF)
+        cross_part = yxr[lax.rem(n, RINGX)]
+        cross_part = dot(perm[1], cross_part) if packed else cross_part.astype(F32)
+        yout[b] = (acc[held(0, n)] + y1r[r].astype(F32) + cross_part).astype(BF)
 
     def down(e, slot):
         tail = jnp.concatenate([wbuf[slot, q * 256:(q + 1) * 256, FF - 256:] for q in range(2)], axis=1)
@@ -219,9 +307,9 @@
 
     def combine(n):
         b = lax.rem(n, 2)
-        send3[b] = dot(ct[3], obuf[3]).astype(BF)
+        send3[b] = dot(ct[3, :rows], obuf[3]).astype(BF)
         send1[b] = dot(ct[1], obuf[1]).astype(BF)
-        acc[held(1, n)] = dot(ct[2], obuf[2])
+        acc[held(1, n)] = dot(ct[2, :rows], obuf[2])
         acc[held(0, n)] = dot(ct[0], obuf[0])
 
     def step(n, _):
@@ -293,7 +381,8 @@
         to1(n).wait_send()
 
     def drain(k, _):
-        cross(k).wait_send()
+        if not packed:
+            cross(k).wait_send()
         side(k).wait_send()
         forward(k).wait_send()
         return 0
@@ -302,13 +391,62 @@
         metas(i).wait_send()
 
 
-def layer(x, u, meta, wg, wu, wd):
+def route(expert, slot, gate, meta, most, mine, got, ssem, rsem):
+    dp, ep = lax.axis_index("dp"), lax.axis_index("ep")
+    ep_of = (ep, (ep // 2) * 2 + (1 - lax.rem(ep, 2)), lax.rem(ep + 2, 4), ((ep // 2) * 2 + (1 - lax.rem(ep, 2)) + 2) % 4)
+    peers = [(lax.rem(dp + i // 4, 2), ep_of[i % 4]) for i in range(1, 8)]
+    barrier = pltpu.get_barrier_semaphore()
+    for a, b in peers:
+        pl.semaphore_signal(barrier, inc=1, device_id={"dp": a, "ep": b}, device_id_type=MESH)
+    which = lax.broadcasted_iota(jnp.int32, (8, TOK), 0)
+    place, weight = jnp.zeros((8, TOK), F32), jnp.zeros((8, TOK), F32)
+    for j in range(2):
+        s = slot[j:j + 1, :]
+        hit = (expert[j:j + 1, :] == which) & (s < SLOTS)
+        place = jnp.where(hit, (s + 1).astype(F32), place)
+        weight = jnp.where(hit, gate[j:j + 1, :].astype(BF).astype(F32), weight)
+    away = jnp.max(jnp.where(which // 4 != ep // 2, place, 0.0), axis=0, keepdims=True)
+    count = jnp.sum(jnp.where(away > 0.0, 1.0, 0.0), axis=1, keepdims=True)
+    mine[...] = jnp.broadcast_to(count, mine.shape)
+    for p in range(4):
+        meta[p, 0:2] = place[2 * p:2 * p + 2]
+        meta[p, 2:4] = weight[2 * p:2 * p + 2]
+        meta[p, 4:8] = jnp.zeros((4, TOK), F32)
+    copies = [pltpu.make_async_remote_copy(
+        src_ref=mine, dst_ref=got.at[i], send_sem=ssem.at[i], recv_sem=rsem.at[i],
+        device_id={"dp": a, "ep": b}, device_id_type=MESH) for i, (a, b) in enumerate(peers)]
+    pl.semaphore_wait(barrier, 7)
+    for c in copies:
+        c.start()
+    top = mine[...]
+    for i, c in enumerate(copies):
+        c.wait_recv()
+        top = jnp.maximum(top, got[i])
+    most[...] = top
+    for c in copies:
+        c.wait_send()
+
+
+def routing(expert, slot, gate):
+    vmem, dma = pltpu.VMEM, pltpu.SemaphoreType.DMA
+    return pl.pallas_call(
+        route,
+        out_shape=(jax.ShapeDtypeStruct((4, 8, TOK), F32), jax.ShapeDtypeStruct((8, 128), F32)),
+        in_specs=[pl.BlockSpec(memory_space=vmem)] * 3,
+        out_specs=(pl.BlockSpec(memory_space=vmem),) * 2,
+        scratch_shapes=[vmem((8, 128), F32), vmem((7, 8, 128), F32), dma((7,)), dma((7,))],
+        compiler_params=pltpu.CompilerParams(collective_id=2, has_side_effects=True),
+        name="route",
+    )(expert, slot, gate)
+
+
+def layer(rows, x, meta, wg, wu, wd):
     hbm, vmem, dma = pl.BlockSpec(memory_space=pl.ANY), pltpu.VMEM, pltpu.SemaphoreType.DMA
-    chunk = (TOK, NC)
+    chunk, part = (TOK, NC), (rows, NC)
     return pl.pallas_call(
-        kernel,
+        functools.partial(kernel, rows),
         out_shape=(jax.ShapeDtypeStruct((TOK, D), BF), jax.ShapeDtypeStruct((3, TOK, D), BF)),
-        in_specs=[hbm] * 6,
+        in_specs=[hbm] * 5,
         out_specs=(hbm, hbm),
         scratch_shapes=[
             vmem((2, 2, ROWS, FF), F32),
@@ -319,35 +457,34 @@
             vmem((4, 2 * SLOTS, TOK), BF),
             vmem((4, TOK, 256), BF),
             vmem((4, 8, TOK), F32),
+            vmem((32, TOK), F32),
+            vmem((3, 8, TOK), F32),
             vmem((4, 256, NC), BF),
+            vmem((2, *part), BF),
             vmem((2, *chunk), BF),
-            vmem((2, *chunk), BF),
-            vmem((2, *chunk), BF),
-            vmem((RING, *chunk), BF),
+            vmem((2, *part), BF),
+            vmem((RING, *part), BF),
             vmem((RING, *chunk), BF),
             vmem((RINGX, *chunk), BF),
             vmem((2, *chunk), BF),
+            vmem((2, TOK, TOK), BF),
             dma((NS, NT // 2 + 2)), dma((2, 4)), dma((2,)), dma((3,)), dma((3,)),
             dma((NK,)), dma((NK,)), dma((NK,)), dma((NK,)), dma((NK,)), dma((NK,)),
             dma((2,)), dma((RING,)), dma((2,)), dma((RING,)), dma((2,)), dma((RINGX,)),
         ],
         compiler_params=pltpu.CompilerParams(
-            collective_id=0, has_side_effects=True, vmem_limit_bytes=67043328),
-        name="moe",
-    )(x, u, meta, wg, wu, wd)
+            collective_id=int(rows < TOK), has_side_effects=True, vmem_limit_bytes=67043328),
+        name=f"moe_{rows}",
+    )(x, meta, wg, wu, wd)[0]
 
 
 def solution(mesh):
     def body(x, expert, slot, gate, wg, wu, wd):
         x = x[0, 0]
-        expert, slot, gate = expert[0, 0], slot[0, 0], gate[0, 0].astype(BF).astype(F32)
-        experts = 2 * mesh.shape["ep"]
-        chosen = (expert.T[None] == jnp.arange(experts)[:, None, None]) & (slot.T[None] < SLOTS)
-        pos = jnp.sum(jnp.where(chosen, slot.T[None] + 1, 0), axis=1).astype(F32) - 1.0
-        weight = jnp.sum(jnp.where(chosen, gate.T[None], 0.0), axis=1)
-        meta = jnp.concatenate(
-            [pos.reshape(-1, 2, TOK), weight.reshape(-1, 2, TOK), jnp.zeros((experts // 2, 4, TOK), F32)], axis=1)
-        return layer(x, x, meta, wg, wu, wd)[0][None, None]
+        meta, most = routing(expert[0, 0].T, slot[0, 0].T, gate[0, 0].T)
+        y = lax.cond(most[0, 0] <= PACKED, functools.partial(layer, PACKED), functools.partial(layer, TOK),
+                     x, meta, wg, wu, wd)
+        return y[None, None]
 
     tok = P("dp", "ep", None, None)
     ex = P("ep", None, None)

time: 228 us -> 208 us (0.912)
  Pallas kernels: 220 us -> 201 us
  other arithmetic: 4.13 us -> 0 us
    pallas_call x1 -> x2, Pallas kernels: 220 us -> 201 us  [the longest x1 193 us: layer(): pl.pallas_call(functools.partial(kernel, rows), out_shape=(jax.ShapeDtype...]
where the time goes in v2:
time: 208 us; the launch traced here: 207 us
  Pallas kernels  201 us (97%)
  local copies, waits for them, and re-layouts  5.31 us (3%)
    pallas_call x1, Pallas kernels, layer(): pl.pallas_call(functools.partial(kernel, rows), out_shape=(jax.ShapeDtype...  193 us
    pallas_call x1, Pallas kernels, routing(): pl.pallas_call(route, out_shape=(jax.ShapeDtypeStruct((4, 8, TOK), F32),...  7.96 us

profile of v2, /device:TPU:0, one launch (start us, length us, event | category | flops | bytes accessed | tf_op | source)
XLA Modules:
  0.0 207.3 jit_solution(14191314968489516428)
XLA Ops:
  0.0 8.0 %route.1 = (f32[4,8,256]{2,1,0:T(8,128)}, f32[8,128]{1,0:T(8,128)}) custom-call(s32[2,256]{1,0:T(2,128)} %bitcast.17, s32[2,256]{1,0:T(2,128)} %bitcast.18, f32[2,256]{1,0:T(2,128)} %bitcast.19), custom_call_target="tpu_custom_call" | custom-call | tf_op jit(solution)/shard_map/route/pallas_call | solution.py:432
  8.0 1.2 slice.3
  9.8 193.4 %conditional.1 = (bf16[1,1,256,7168]{3,2,1,0:T(8,128)(2,1)}) conditional(s32[]{:T(128)} %bitcast.8, (bf16[256,7168]{1,0:T(8,128)(2,1)}, f32[4,8,256]{2,1,0:T(8,128)}, bf16[2,7168,4864]{2,1,0:T(8,128)(2,1)}, bf16[2,7168,4864]{2,1,0:T(8,128)(2,1)}, bf16[2,4864,7168]{2,1,0:T(8,128)(2,1)}) %tuple.16, (bf16[256,7168]{1,0:T(8,128)(2,1)}, ...), branch_computations={%region_0.0_spmd, %region_1.0_spmd} | conditional | bytes 8 | solution.py:485
  10.0 192.9 %moe_176.1 = (bf16[256,7168]{1,0:T(8,128)(2,1)}, bf16[3,256,7168]{2,1,0:T(8,128)(2,1)}) custom-call(bf16[256,7168]{1,0:T(8,128)(2,1)} %get-tuple-element.34.x, f32[4,8,256]{2,1,0:T(8,128)} %get-tuple-element.35.meta, bf16[2,7168,4864]{2,1,0:T(8,128)(2,1)} %get-tuple-element.36.wg, bf16[2,7168,4864]{2,1,0:T(8,128)(2,1)} %get-tuple-element.37.wu, ...), custom_call_target="tpu_custom_call" | custom-call | tf_op jit(solution)/shard_map/cond/branch_1_fun/moe_176/pallas_call | solution.py:446
  203.2 4.1 %copy.13 = bf16[1,1,256,7168]{3,2,1,0:T(8,128)(2,1)} copy(bf16[1,1,256,7168]{3,2,1,0:T(8,128)(2,1)} %get-tuple-element.44) | data formatting | bytes 7340032

commit v3 on v2

--- a/solution.py
+++ b/solution.py
@@ -19,7 +19,7 @@
 LAG = 3
 RING = 4
 RINGX = 5
-PACKED = 176
+PACKED = 160
 BF, F32 = jnp.bfloat16, jnp.float32
 
 

time: 208 us -> 207 us (level)
  no operation moved by 1% of the time
where the time goes in v3:
time: 207 us; the launch traced here: 206 us
  Pallas kernels  200 us (97%)
  local copies, waits for them, and re-layouts  5.31 us (3%)
    pallas_call x1, Pallas kernels, layer(): pl.pallas_call(functools.partial(kernel, rows), out_shape=(jax.ShapeDtype...  192 us
    pallas_call x1, Pallas kernels, routing(): pl.pallas_call(route, out_shape=(jax.ShapeDtypeStruct((4, 8, TOK), F32),...  7.96 us

profile of v3, /device:TPU:0, one launch (start us, length us, event | category | flops | bytes accessed | tf_op | source)
XLA Modules:
  0.0 206.3 jit_solution(2084749451592460393)
XLA Ops:
  0.0 8.0 %route.1 = (f32[4,8,256]{2,1,0:T(8,128)}, f32[8,128]{1,0:T(8,128)}) custom-call(s32[2,256]{1,0:T(2,128)} %bitcast.17, s32[2,256]{1,0:T(2,128)} %bitcast.18, f32[2,256]{1,0:T(2,128)} %bitcast.19), custom_call_target="tpu_custom_call" | custom-call | tf_op jit(solution)/shard_map/route/pallas_call | solution.py:432
  8.0 1.2 slice.3
  9.8 192.4 %conditional.1 = (bf16[1,1,256,7168]{3,2,1,0:T(8,128)(2,1)}) conditional(s32[]{:T(128)} %bitcast.8, (bf16[256,7168]{1,0:T(8,128)(2,1)}, f32[4,8,256]{2,1,0:T(8,128)}, bf16[2,7168,4864]{2,1,0:T(8,128)(2,1)}, bf16[2,7168,4864]{2,1,0:T(8,128)(2,1)}, bf16[2,4864,7168]{2,1,0:T(8,128)(2,1)}) %tuple.16, (bf16[256,7168]{1,0:T(8,128)(2,1)}, ...), branch_computations={%region_0.0_spmd, %region_1.0_spmd} | conditional | bytes 8 | solution.py:485
  10.0 191.9 %moe_160.1 = (bf16[256,7168]{1,0:T(8,128)(2,1)}, bf16[3,256,7168]{2,1,0:T(8,128)(2,1)}) custom-call(bf16[256,7168]{1,0:T(8,128)(2,1)} %get-tuple-element.34.x, f32[4,8,256]{2,1,0:T(8,128)} %get-tuple-element.35.meta, bf16[2,7168,4864]{2,1,0:T(8,128)(2,1)} %get-tuple-element.36.wg, bf16[2,7168,4864]{2,1,0:T(8,128)(2,1)} %get-tuple-element.37.wu, ...), custom_call_target="tpu_custom_call" | custom-call | tf_op jit(solution)/shard_map/cond/branch_1_fun/moe_160/pallas_call | solution.py:446
  202.2 4.1 %copy.13 = bf16[1,1,256,7168]{3,2,1,0:T(8,128)(2,1)} copy(bf16[1,1,256,7168]{3,2,1,0:T(8,128)(2,1)} %get-tuple-element.44) | data formatting | bytes 7340032
